TPU v7x, 8 devices: a whole 2x2x1 slice. The times are simulated.
8 devices in a mesh: rows: 2 (over z, y), terms: 4 (over x, core).
Axes of the slice: x: 2, y: 2, z: 1, core: 2. Of those that a mesh axis runs over, the one named last changes fastest.
Arguments:
- psi_init: float32 [768, 4, 4, 768], P(('rows', 'terms'))
- left_env: bfloat16 [24, 768, 768], P('terms', 'rows')
- two_site: bfloat16 [24, 16, 16], P('terms')
- right_env: bfloat16 [24, 768, 768], P('terms')
Outputs:
- output 1: float32 [7, 768, 4, 4, 768], P(None, ('rows', 'terms'))
- output 2: float32 [6], replicated
- output 3: float32 [6], replicated
All inputs are finite; a program needn't handle non-finite values.
Results may differ from a plain program's by a relative error of at most 0.02.
Values are sent between devices in bfloat16 or wider.
A program may use at most 1 GiB of HBM per device.

v0:
```python
import jax
import jax.numpy as jnp
from jax import lax
from jax.sharding import PartitionSpec as P

STEPS = 6


def solution(mesh):
    all_axes = ("rows", "terms")
    dev_total = mesh.shape["rows"] * mesh.shape["terms"]

    def local_run(psi_blk, left_env, two_site, right_env):
        elem_count = psi_blk.size * dev_total
        term_local, slab_rows, bond_dim = left_env.shape
        phys_pair = psi_blk.shape[1] * psi_blk.shape[2]
        left_flat = left_env.reshape(term_local * slab_rows, bond_dim)

        def inner_mean(x_vec, y_vec):
            return lax.psum(jnp.sum(x_vec * y_vec), all_axes) / elem_count

        def matvec(cur_blk):
            whole_vec = lax.all_gather(cur_blk.astype(jnp.bfloat16), all_axes, axis=0, tiled=True)
            flat_vec = whole_vec.reshape(bond_dim, phys_pair * bond_dim)
            left_out = jnp.dot(left_flat, flat_vec, preferred_element_type=jnp.float32)
            left_out = left_out.astype(jnp.bfloat16).reshape(term_local, slab_rows, phys_pair, bond_dim)
            phys_out = lax.dot_general(left_out, two_site, (((2,), (2,)), ((0,), (0,))), preferred_element_type=jnp.float32).astype(jnp.bfloat16)
            part_sum = lax.dot_general(phys_out, right_env, (((0, 2), (0, 2)), ((), ())), preferred_element_type=jnp.float32)
            summed = lax.psum_scatter(part_sum, "terms", scatter_dimension=0, tiled=True)
            return summed.reshape(cur_blk.shape)

        cur_vec = psi_blk / jnp.sqrt(inner_mean(psi_blk, psi_blk))
        prev_vec = cur_vec
        beta_prev = None
        vectors = [cur_vec]
        alpha_list = []
        beta_list = []
        for step_idx in range(STEPS):
            w_vec = matvec(cur_vec)
            alpha_j = inner_mean(w_vec, cur_vec)
            w_vec = w_vec - alpha_j * cur_vec
            if step_idx > 0:
                w_vec = w_vec - beta_prev * prev_vec
            beta_j = jnp.sqrt(inner_mean(w_vec, w_vec))
            prev_vec = cur_vec
            cur_vec = w_vec / beta_j
            beta_prev = beta_j
            vectors.append(cur_vec)
            alpha_list.append(alpha_j)
            beta_list.append(beta_j)
        return jnp.stack(vectors), jnp.stack(alpha_list), jnp.stack(beta_list)

    return jax.shard_map(local_run, mesh=mesh, in_specs=(P(all_axes), P("terms", "rows"), P("terms"), P("terms")), out_specs=(P(None, all_axes), P(), P()), check_vma=False)
```

profile of v0, /device:TPU:0, one launch (start us, length us, event | category | flops | bytes accessed | tf_op | source)
XLA Modules:
  0.0 3642.7 jit_solution(15257094217139928978)
XLA Ops:
  43.7 93.9 %all-gather.7.cloned.1.call-done = bf16[768,4,4,768]{3,2,1,0:T(4,128)(2,1)} async-done(((bf16[96,4,4,768]{3,2,1,0:T(4,128)(2,1)}), bf16[768,4,4,768]{3,2,1,0:T(4,128)(2,1)}) %all-gather.7.cloned.1.call-update) | async-done | bytes 18874384 | tf_op jit(solution)/shard_map/all_gather | solution.py:23
  166.7 56.5 %fusion = bf16[2304,12288]{0,1:T(8,128)(2,1)} fusion(bf16[768,12288]{1,0:T(8,128)(2,1)} %reshape.63, bf16[2304,768]{1,0:T(8,128)(2,1)S(1)} %bitcast.200), kind=kOutput, calls=%fused_computation.6 | convolution fusion | flops 43514855424 | bytes 79036416 | tf_op jit(solution)/shard_map/dot_general | solution.py:25
  223.2 65.7 %copy.37 = bf16[2304,12288]{1,0:T(8,128)(2,1)} copy(bf16[2304,12288]{0,1:T(8,128)(2,1)} %fusion) | data formatting | bytes 113246208 | tf_op jit(solution)/shard_map/convert_element_type | solution.py:26
  367.1 52.6 %fusion.28 = f32[384,16,768,1]{2,1,0,3:T(8,128)} fusion(bf16[6,768,768]{2,1,0:T(8,128)(2,1)} %param.7, bf16[6,384,768,16]{2,3,1,0:T(8,128)(2,1)} %fusion.119), kind=kOutput, calls=%fused_computation.34 | convolution fusion | flops 43486543872 | bytes 82575360 | tf_op jit(solution)/shard_map/dot_general | solution.py:28
  437.2 131.5 %reduce-scatter.7.cloned.1.call-done = f32[96,16,768]{2,0,1:T(8,128)} async-done(((f32[384,16,768]{2,0,1:T(8,128)}), f32[96,16,768]{2,0,1:T(8,128)}) %reduce-scatter.7.cloned.1.call-update) | async-done | bytes 4718608 | tf_op jit(solution)/shard_map/reduce_scatter | solution.py:29
  643.4 94.1 %all-gather.9.cloned.1.call-done = bf16[768,4,4,768]{3,2,1,0:T(4,128)(2,1)} async-done(((bf16[96,4,4,768]{3,2,1,0:T(4,128)(2,1)}), bf16[768,4,4,768]{3,2,1,0:T(4,128)(2,1)}) %all-gather.9.cloned.1.call-update) | async-done | bytes 18874384 | tf_op jit(solution)/shard_map/all_gather | solution.py:23
  766.8 56.5 %fusion.1 = bf16[2304,12288]{0,1:T(8,128)(2,1)} fusion(bf16[768,12288]{1,0:T(8,128)(2,1)} %reshape.67, bf16[2304,768]{1,0:T(8,128)(2,1)S(1)} %bitcast.201), kind=kOutput, calls=%fused_computation.7 | convolution fusion | flops 43514855424 | bytes 79036416 | tf_op jit(solution)/shard_map/dot_general | solution.py:25
  823.3 65.7 %copy.41 = bf16[2304,12288]{1,0:T(8,128)(2,1)} copy(bf16[2304,12288]{0,1:T(8,128)(2,1)} %fusion.1) | data formatting | bytes 113246208 | tf_op jit(solution)/shard_map/convert_element_type | solution.py:26
  967.2 52.5 %fusion.26 = f32[384,16,768,1]{2,1,0,3:T(8,128)} fusion(bf16[6,768,768]{2,1,0:T(8,128)(2,1)} %param.7, bf16[6,384,768,16]{2,3,1,0:T(8,128)(2,1)} %fusion.115), kind=kOutput, calls=%fused_computation.32 | convolution fusion | flops 43486543872 | bytes 82575360 | tf_op jit(solution)/shard_map/dot_general | solution.py:28
  1037.3 131.5 %reduce-scatter.9.cloned.1.call-done = f32[96,16,768]{2,0,1:T(8,128)} async-done(((f32[384,16,768]{2,0,1:T(8,128)}), f32[96,16,768]{2,0,1:T(8,128)}) %reduce-scatter.9.cloned.1.call-update) | async-done | bytes 4718608 | tf_op jit(solution)/shard_map/reduce_scatter | solution.py:29
  1240.5 94.1 %all-gather.11.cloned.1.call-done = bf16[768,4,4,768]{3,2,1,0:T(4,128)(2,1)} async-done(((bf16[96,4,4,768]{3,2,1,0:T(4,128)(2,1)}), bf16[768,4,4,768]{3,2,1,0:T(4,128)(2,1)}) %all-gather.11.cloned.1.call-update) | async-done | bytes 18874384 | tf_op jit(solution)/shard_map/all_gather | solution.py:23
  1363.7 56.5 %fusion.2 = bf16[2304,12288]{0,1:T(8,128)(2,1)} fusion(bf16[768,12288]{1,0:T(8,128)(2,1)} %reshape.70, bf16[2304,768]{1,0:T(8,128)(2,1)S(1)} %bitcast.202), kind=kOutput, calls=%fused_computation.8 | convolution fusion | flops 43514855424 | bytes 79036416 | tf_op jit(solution)/shard_map/dot_general | solution.py:25
  1420.1 65.7 %copy.45 = bf16[2304,12288]{1,0:T(8,128)(2,1)} copy(bf16[2304,12288]{0,1:T(8,128)(2,1)} %fusion.2) | data formatting | bytes 113246208 | tf_op jit(solution)/shard_map/convert_element_type | solution.py:26
  1564.1 52.5 %fusion.24 = f32[384,16,768,1]{2,1,0,3:T(8,128)} fusion(bf16[6,768,768]{2,1,0:T(8,128)(2,1)} %param.7, bf16[6,384,768,16]{2,3,1,0:T(8,128)(2,1)} %fusion.111), kind=kOutput, calls=%fused_computation.30 | convolution fusion | flops 43486543872 | bytes 82575360 | tf_op jit(solution)/shard_map/dot_general | solution.py:28
  1634.1 131.5 %reduce-scatter.11.cloned.1.call-done = f32[96,16,768]{2,0,1:T(8,128)} async-done(((f32[384,16,768]{2,0,1:T(8,128)}), f32[96,16,768]{2,0,1:T(8,128)}) %reduce-scatter.11.cloned.1.call-update) | async-done | bytes 4718608 | tf_op jit(solution)/shard_map/reduce_scatter | solution.py:29
  1837.3 94.1 %all-gather.13.cloned.1.call-done = bf16[768,4,4,768]{3,2,1,0:T(4,128)(2,1)} async-done(((bf16[96,4,4,768]{3,2,1,0:T(4,128)(2,1)}), bf16[768,4,4,768]{3,2,1,0:T(4,128)(2,1)}) %all-gather.13.cloned.1.call-update) | async-done | bytes 18874384 | tf_op jit(solution)/shard_map/all_gather | solution.py:23
  1960.5 56.5 %fusion.3 = bf16[2304,12288]{0,1:T(8,128)(2,1)} fusion(bf16[768,12288]{1,0:T(8,128)(2,1)} %reshape.73, bf16[2304,768]{1,0:T(8,128)(2,1)S(1)} %bitcast.203), kind=kOutput, calls=%fused_computation.9 | convolution fusion | flops 43514855424 | bytes 79036416 | tf_op jit(solution)/shard_map/dot_general | solution.py:25
  2017.0 65.7 %copy.49 = bf16[2304,12288]{1,0:T(8,128)(2,1)} copy(bf16[2304,12288]{0,1:T(8,128)(2,1)} %fusion.3) | data formatting | bytes 113246208 | tf_op jit(solution)/shard_map/convert_element_type | solution.py:26
  2160.9 52.8 %fusion.22 = f32[384,16,768,1]{2,1,0,3:T(8,128)} fusion(bf16[6,768,768]{2,1,0:T(8,128)(2,1)} %param.7, bf16[6,384,768,16]{2,3,1,0:T(8,128)(2,1)} %fusion.107), kind=kOutput, calls=%fused_computation.28 | convolution fusion | flops 43486543872 | bytes 82575360 | tf_op jit(solution)/shard_map/dot_general | solution.py:28
  2231.3 131.5 %reduce-scatter.13.cloned.1.call-done = f32[96,16,768]{2,0,1:T(8,128)} async-done(((f32[384,16,768]{2,0,1:T(8,128)}), f32[96,16,768]{2,0,1:T(8,128)}) %reduce-scatter.13.cloned.1.call-update) | async-done | bytes 4718608 | tf_op jit(solution)/shard_map/reduce_scatter | solution.py:29
  2434.4 94.1 %all-gather.15.cloned.1.call-done = bf16[768,4,4,768]{3,2,1,0:T(4,128)(2,1)} async-done(((bf16[96,4,4,768]{3,2,1,0:T(4,128)(2,1)}), bf16[768,4,4,768]{3,2,1,0:T(4,128)(2,1)}) %all-gather.15.cloned.1.call-update) | async-done | bytes 18874384 | tf_op jit(solution)/shard_map/all_gather | solution.py:23
  2557.6 56.5 %fusion.4 = bf16[2304,12288]{0,1:T(8,128)(2,1)} fusion(bf16[768,12288]{1,0:T(8,128)(2,1)} %reshape.76, bf16[2304,768]{1,0:T(8,128)(2,1)S(1)} %bitcast.204), kind=kOutput, calls=%fused_computation.10 | convolution fusion | flops 43514855424 | bytes 79036416 | tf_op jit(solution)/shard_map/dot_general | solution.py:25
  2614.1 65.7 %copy.53 = bf16[2304,12288]{1,0:T(8,128)(2,1)} copy(bf16[2304,12288]{0,1:T(8,128)(2,1)} %fusion.4) | data formatting | bytes 113246208 | tf_op jit(solution)/shard_map/convert_element_type | solution.py:26
  2717.9 40.1 %fusion.103 = bf16[6,384,768,16]{2,3,1,0:T(8,128)(2,1)} fusion(bf16[6,16,16]{2,1,0:T(8,128)(2,1)} %param.6, bf16[6,384,16,768]{3,2,1,0:T(8,128)(2,1)} %bitcast.216), kind=kOutput, calls=%fused_computation.27.clone | convolution fusion | flops 934281216 | bytes 113249280 | tf_op jit(solution)/shard_map/dot_general | solution.py:27
  2758.0 52.7 %fusion.20 = f32[384,16,768,1]{2,1,0,3:T(8,128)} fusion(bf16[6,768,768]{2,1,0:T(8,128)(2,1)} %param.7, bf16[6,384,768,16]{2,3,1,0:T(8,128)(2,1)} %fusion.103), kind=kOutput, calls=%fused_computation.26 | convolution fusion | flops 43486543872 | bytes 82575360 | tf_op jit(solution)/shard_map/dot_general | solution.py:28
  2828.3 131.5 %reduce-scatter.15.cloned.1.call-done = f32[96,16,768]{2,0,1:T(8,128)} async-done(((f32[384,16,768]{2,0,1:T(8,128)}), f32[96,16,768]{2,0,1:T(8,128)}) %reduce-scatter.15.cloned.1.call-update) | async-done | bytes 4718608 | tf_op jit(solution)/shard_map/reduce_scatter | solution.py:29
  3031.4 94.1 %all-gather.17.cloned.1.call-done = bf16[768,4,4,768]{3,2,1,0:T(4,128)(2,1)} async-done(((bf16[96,4,4,768]{3,2,1,0:T(4,128)(2,1)}), bf16[768,4,4,768]{3,2,1,0:T(4,128)(2,1)}) %all-gather.17.cloned.1.call-update) | async-done | bytes 18874384 | tf_op jit(solution)/shard_map/all_gather | solution.py:23
  3154.6 56.5 %fusion.5 = bf16[2304,12288]{0,1:T(8,128)(2,1)} fusion(bf16[768,12288]{1,0:T(8,128)(2,1)} %reshape.79, bf16[2304,768]{1,0:T(8,128)(2,1)S(1)} %bitcast.205), kind=kOutput, calls=%fused_computation.11 | convolution fusion | flops 43514855424 | bytes 79036416 | tf_op jit(solution)/shard_map/dot_general | solution.py:25
  3211.1 65.7 %copy.57 = bf16[2304,12288]{1,0:T(8,128)(2,1)} copy(bf16[2304,12288]{0,1:T(8,128)(2,1)} %fusion.5) | data formatting | bytes 113246208 | tf_op jit(solution)/shard_map/convert_element_type | solution.py:26
  3314.9 40.1 %fusion.99 = bf16[6,384,768,16]{2,3,1,0:T(8,128)(2,1)} fusion(bf16[6,16,16]{2,1,0:T(8,128)(2,1)} %param.6, bf16[6,384,16,768]{3,2,1,0:T(8,128)(2,1)} %bitcast.217), kind=kOutput, calls=%fused_computation.25.clone.1 | convolution fusion | flops 934281216 | bytes 113249280 | tf_op jit(solution)/shard_map/dot_general | solution.py:27
  3355.0 52.5 %fusion.18 = f32[384,16,768,1]{2,1,0,3:T(8,128)} fusion(bf16[6,768,768]{2,1,0:T(8,128)(2,1)} %param.7, bf16[6,384,768,16]{2,3,1,0:T(8,128)(2,1)} %fusion.99), kind=kOutput, calls=%fused_computation.24 | convolution fusion | flops 43486543872 | bytes 82575360 | tf_op jit(solution)/shard_map/dot_general | solution.py:28
  3446.1 110.5 %reduce-scatter.17.cloned.1.call-done = f32[96,16,768]{2,0,1:T(8,128)} async-done(((f32[384,16,768]{2,0,1:T(8,128)}), f32[96,16,768]{2,0,1:T(8,128)}) %reduce-scatter.17.cloned.1.call-update) | async-done | bytes 4718608 | tf_op jit(solution)/shard_map/reduce_scatter | solution.py:29
  (101 shorter events, 1158.2 us)
Async XLA Ops:
  7.2 159.5 %copy-start = (bf16[6,384,768]{2,1,0:T(8,128)(2,1)S(1)}, bf16[6,384,768]{2,1,0:T(8,128)(2,1)}, u32[]{:S(2)}) copy-start(bf16[6,384,768]{2,1,0:T(8,128)(2,1)} %param.5) | copy-start | bytes 10616836
  7.2 130.4 %all-gather.7.cloned.1.call-start = ((), (), s32[]{:S(2)}) async-start(), calls=%async_computation.6 | async-start | bytes 21233664 | tf_op jit(solution)/shard_map/all_gather | solution.py:23
  43.5 525.3 %reduce-scatter.7.cloned.1.call-start = ((), (), s32[]{:S(2)}) async-start(), calls=%async_computation.7 | async-start | bytes 23592960 | tf_op jit(solution)/shard_map/reduce_scatter | solution.py:29
  437.2 300.3 %all-gather.9.cloned.1.call-start = ((), (), s32[]{:S(2)}) async-start(), calls=%async_computation.8 | async-start | bytes 21233664 | tf_op jit(solution)/shard_map/all_gather | solution.py:23
  643.4 525.4 %reduce-scatter.9.cloned.1.call-start = ((), (), s32[]{:S(2)}) async-start(), calls=%async_computation.9 | async-start | bytes 23592960 | tf_op jit(solution)/shard_map/reduce_scatter | solution.py:29
  1037.2 297.3 %all-gather.11.cloned.1.call-start = ((), (), s32[]{:S(2)}) async-start(), calls=%async_computation.10 | async-start | bytes 21233664 | tf_op jit(solution)/shard_map/all_gather | solution.py:23
  1240.4 525.3 %reduce-scatter.11.cloned.1.call-start = ((), (), s32[]{:S(2)}) async-start(), calls=%async_computation.11 | async-start | bytes 23592960 | tf_op jit(solution)/shard_map/reduce_scatter | solution.py:29
  1634.1 297.3 %all-gather.13.cloned.1.call-start = ((), (), s32[]{:S(2)}) async-start(), calls=%async_computation.12 | async-start | bytes 21233664 | tf_op jit(solution)/shard_map/all_gather | solution.py:23
  1837.2 525.6 %reduce-scatter.13.cloned.1.call-start = ((), (), s32[]{:S(2)}) async-start(), calls=%async_computation.13 | async-start | bytes 23592960 | tf_op jit(solution)/shard_map/reduce_scatter | solution.py:29
  2231.2 297.2 %all-gather.15.cloned.1.call-start = ((), (), s32[]{:S(2)}) async-start(), calls=%async_computation.14 | async-start | bytes 21233664 | tf_op jit(solution)/shard_map/all_gather | solution.py:23
  2434.3 525.5 %reduce-scatter.15.cloned.1.call-start = ((), (), s32[]{:S(2)}) async-start(), calls=%async_computation.15 | async-start | bytes 23592960 | tf_op jit(solution)/shard_map/reduce_scatter | solution.py:29
  2828.3 297.2 %all-gather.17.cloned.1.call-start = ((), (), s32[]{:S(2)}) async-start(), calls=%async_computation.16 | async-start | bytes 21233664 | tf_op jit(solution)/shard_map/all_gather | solution.py:23
  3031.3 525.3 %reduce-scatter.17.cloned.1.call-start = ((), (), s32[]{:S(2)}) async-start(), calls=%async_computation.17 | async-start | bytes 23592960 | tf_op jit(solution)/shard_map/reduce_scatter | solution.py:29
  3425.1 5.8 copy-start.1
  3430.8 8.8 slice-start
  3433.9 5.7 slice-start.1
  3433.9 9.0 slice-start.2
  3439.7 3.2 slice-start.3
Sparse Core Ops, SparseCore 0:
  43.6 93.9 all-gather.6
  437.3 131.4 reduce-scatter.6
  643.5 93.9 all-gather.8
  1037.4 131.3 reduce-scatter.8
  1240.6 93.9 all-gather.10
  1634.2 131.4 reduce-scatter.10
  1837.4 93.9 all-gather.12
  2231.4 131.4 reduce-scatter.12
  2434.5 93.9 all-gather.14
  2828.4 131.3 reduce-scatter.14
  3031.5 93.9 all-gather.16
  3425.2 131.3 reduce-scatter.16
where the time goes:
time: 3660 us; the launch traced here: 3640 us
  waiting for transfers between devices  1330 us (36%)
  local copies, waits for them, and re-layouts  907 us (25%)
  matrix products  895 us (24%)
  blocking collectives  307 us (8%)
  other arithmetic  176 us (5%)
    reduce_scatter x6, waiting for transfers between devices, matvec(): lax.psum_scatter(part_sum, 'terms', scatter_dimension=0, tiled=True)  768 us
    all_gather x6, waiting for transfers between devices, matvec(): lax.all_gather(cur_blk.astype(jnp.bfloat16), all_axes, axis=0, tiled=True)  564 us
    convert_element_type x6, local copies, waits for them, and re-layouts, matvec(): left_out.astype(jnp.bfloat16)  394 us
    dot_general x6, matrix products, matvec(): left_out = jnp.dot(left_flat, flat_vec, preferred_element_type=jnp.float32)  339 us
    dot_general x6, matrix products, matvec(): lax.dot_general(phys_out, right_env, (((0, 2), (0, 2)), ((), ())), prefer...  316 us
    psum x13, blocking collectives, inner_mean(): return lax.psum(jnp.sum(x_vec * y_vec), all_axes) / elem_count  307 us
    dot_general x6, matrix products, matvec(): lax.dot_general(left_out, two_site, (((2,), (2,)), ((0,), (0,))), preferr...  241 us
    unnamed x19, local copies, waits for them, and re-layouts  232 us
  transfers between devices with their start and end apart: 12, of which 12 were waited for; matrix products, arithmetic and copies ran while one was open for 1% of the time, Pallas kernels for 0%

commit v1 on v0

v1 whole, which is shorter than its diff:
```python
import functools

import jax
import jax.numpy as jnp
from jax import lax
from jax.experimental import pallas as pl
from jax.experimental.pallas import tpu as pltpu
from jax.sharding import PartitionSpec as P

STEPS = 6
MESH = pl.DeviceIdType.MESH
BF = jnp.bfloat16
F32 = jnp.float32
LANE = 128
SEND_O, SEND_F, SEND_P, FWD_D, FWD_PO, FWD_PF, FWD_PD = range(7)
R_OWN, R_X, R_Y, R_PX, R_PY = range(5)


def lanczos_kernel(psi_ref, left_ref, kron_ref, right_ref, out_ref, ab_ref, rbuf,
                   vecs, uvec, lvm, kvm, rvm, xbuf, ybuf, sums, beta_s,
                   load_sem, rload_sem, out_sem, u_send, u_recv, r_send, r_recv,
                   l_send, l_recv, s_send, s_recv):
    group_terms, _, bond = left_ref.shape
    phys, slab, _ = psi_ref.shape
    chunks = bond // LANE
    groups = 4
    elem_count = phys * bond * bond
    half_terms = group_terms // 2

    r = lax.axis_index("rows")
    t = lax.axis_index("terms")
    c = t % 2
    x = t // 2
    me = r * 4 + t
    xn = (1 - x) * 2 + c
    part_t = t + 1 - 2 * c
    xnp = xn + 1 - 2 * c
    f_dev = (r + (1 - c) * (1 - 2 * r), t + c * (xn - t))
    o_dev = (r + c * (1 - 2 * r), t + (1 - c) * (xn - t))
    d_dev = (1 - r, xn)
    p_dev = (r, part_t)
    y_dev = (1 - r, t)
    x_dev = (r, xn)

    def block_of(dev):
        return dev[0] * 4 + dev[1]

    def rows_of(block):
        return pl.ds(pl.multiple_of(block * slab, 16), slab)

    def remote(src, dst, ssem, rsem, dev):
        return pltpu.make_async_remote_copy(src_ref=src, dst_ref=dst, send_sem=ssem, recv_sem=rsem,
                                            device_id=dev, device_id_type=MESH)

    def u_copy(kind, ci):
        block = {SEND_O: block_of((r, t)), SEND_F: block_of((r, t)), SEND_P: block_of((r, t)),
                 FWD_D: block_of(o_dev), FWD_PO: block_of(o_dev),
                 FWD_PF: block_of(f_dev), FWD_PD: block_of(d_dev)}[kind]
        dev = {SEND_O: o_dev, SEND_F: f_dev, SEND_P: p_dev, FWD_D: f_dev,
               FWD_PO: p_dev, FWD_PF: p_dev, FWD_PD: p_dev}[kind]
        ref = uvec.at[ci, :, rows_of(block), :]
        return remote(ref, ref, u_send.at[kind, ci], u_recv.at[kind, ci], dev)

    def r_copy(kind, ci):
        rows = pl.ds(pl.multiple_of(ci * LANE, LANE), LANE)
        mine = pl.ds(r * half_terms, half_terms)
        other = pl.ds((1 - r) * half_terms, half_terms)
        src, dst, dev = {
            R_OWN: (right_ref.at[:, rows, :], rbuf.at[0, :, rows, :], p_dev),
            R_X: (right_ref.at[mine, rows, :], rbuf.at[1, mine, rows, :], x_dev),
            R_Y: (rbuf.at[1, mine, rows, :], rbuf.at[1, mine, rows, :], y_dev),
            R_PX: (rbuf.at[1, mine, rows, :], rbuf.at[2, mine, rows, :], p_dev),
            R_PY: (rbuf.at[1, other, rows, :], rbuf.at[2, other, rows, :], p_dev),
        }[kind]
        return remote(src, dst, r_send.at[kind, ci], r_recv.at[kind, ci], dev)

    def l_copy(g):
        tgt = (part_t, xn, xnp)[g]
        return remote(left_ref.at[:, rows_of(tgt), :], lvm.at[g + 1], l_send.at[g], l_recv.at[g], (r, tgt))

    def r_load(ci, kg, slot):
        rows = pl.ds(pl.multiple_of(ci * LANE, LANE), LANE)

        @pl.when(kg == 0)
        def _():
            pltpu.make_async_copy(right_ref.at[:, rows, :], rvm.at[slot], rload_sem.at[slot]).start()

        @pl.when(kg != 0)
        def _():
            pltpu.make_async_copy(rbuf.at[jnp.maximum(kg - 1, 0), :, rows, :], rvm.at[slot], rload_sem.at[slot]).start()

    def r_load_wait(slot):
        pltpu.make_async_copy(right_ref.at[:, pl.ds(0, LANE), :], rvm.at[slot], rload_sem.at[slot]).wait()

    def sum_copy(kind, rel):
        tgt = (me + rel) % 8
        ref = sums.at[kind, me]
        return remote(ref, ref, s_send.at[kind, rel - 1], s_recv.at[kind, rel - 1], (tgt // 4, tgt % 4))

    def all_mean(kind, partial):
        sums[kind, pl.ds(me, 1)] = partial[None]
        for rel in range(1, 8):
            sum_copy(kind, rel).start()
        for rel in range(1, 8):
            sum_copy(kind, rel).wait()
        tile = jnp.sum(sums[kind], axis=0)
        total = jnp.sum(jnp.sum(tile, axis=0, keepdims=True), axis=1, keepdims=True)
        return total / elem_count

    def fold_tiles(arr):
        acc = jnp.zeros((8, LANE), F32)
        for i in range(slab // 8):
            for j in range(bond // LANE):
                acc = acc + arr[i * 8:i * 8 + 8, j * LANE:j * LANE + LANE]
        return acc

    def norm_and_pack(slot, scale, pack):
        def one_chunk(ci):
            lanes = pl.ds(pl.multiple_of(ci * LANE, LANE), LANE)

            def one_q(qp, _):
                for h in range(2):
                    val = vecs[slot, 2 * qp + h, :, lanes] * scale
                    vecs[slot, 2 * qp + h, :, lanes] = val
                    if pack:
                        uvec[ci, qp, rows_of(me), h * LANE:(h + 1) * LANE] = val.astype(BF)
                return 0
            lax.fori_loop(0, phys // 2, one_q, 0)
        if pack:
            one_chunk(0)
            one_chunk(1)
            for kind in (SEND_O, SEND_F, SEND_P):
                u_copy(kind, 0).start()
            u_copy(SEND_O, 1).start()

            def rest(ci, _):
                one_chunk(ci)
                return 0
            lax.fori_loop(2, chunks, rest, 0)
        else:
            def every(ci, _):
                one_chunk(ci)
                return 0
            lax.fori_loop(0, chunks, every, 0)

    def out_copy(slot, idx):
        return pltpu.make_async_copy(vecs.at[slot], out_ref.at[idx], out_sem.at[slot])

    barrier = pltpu.get_barrier_semaphore()
    for rel in range(1, 8):
        tgt = (me + rel) % 8
        pl.semaphore_signal(barrier, inc=1, device_id=(tgt // 4, tgt % 4), device_id_type=MESH)
    psi_load = pltpu.make_async_copy(psi_ref, vecs.at[0], load_sem.at[0])
    psi_load.start()
    kron_load = pltpu.make_async_copy(kron_ref, kvm, load_sem.at[1])
    kron_load.start()
    own_left = pltpu.make_async_copy(left_ref.at[:, rows_of(t), :], lvm.at[0], load_sem.at[2])
    own_left.start()
    pl.semaphore_wait(barrier, 7)
    r_copy(R_X, 0).start()
    r_copy(R_OWN, 0).start()
    for g in range(3):
        l_copy(g).start()
    r_load(0, 0, 0)
    psi_load.wait()

    def sq_q(q, acc):
        val = vecs[0, q]
        return acc + fold_tiles(val * val)
    norm = jnp.sqrt(all_mean(1, lax.fori_loop(0, phys, sq_q, jnp.zeros((8, LANE), F32))))
    norm_and_pack(0, 1.0 / norm, True)
    r_copy(R_X, 1).start()
    r_copy(R_OWN, 1).start()
    out_copy(0, 0).start()
    r_copy(R_X, 0).wait_recv()
    r_copy(R_Y, 0).start()
    r_copy(R_PX, 0).start()
    beta_s[...] = jnp.zeros_like(beta_s)
    kron_load.wait()
    own_left.wait()

    def step_body(step, _):
        cur = step % 3
        prev = (step + 2) % 3
        nxt = (step + 1) % 3

        @pl.when(step >= 2)
        def _():
            out_copy(nxt, step - 2).wait()

        def zero_q(q, _):
            vecs[nxt, q] = jnp.zeros((slab, bond), F32)
            return 0
        lax.fori_loop(0, phys, zero_q, 0)

        u_copy(SEND_O, 0).wait_recv()
        u_copy(FWD_D, 0).start()
        u_copy(FWD_PO, 0).start()
        u_copy(SEND_F, 1).start()
        u_copy(SEND_P, 1).start()

        @pl.when(step == 0)
        def _():
            r_copy(R_Y, 0).wait_recv()
            r_copy(R_PY, 0).start()
        u_copy(SEND_F, 0).wait_recv()
        u_copy(FWD_PF, 0).start()
        u_copy(FWD_D, 0).wait_recv()
        u_copy(FWD_PD, 0).start()

        def iteration(it, _):
            ci = it // groups
            kg = it % groups
            slot = it % 2
            first = step == 0

            @pl.when(kg == 0)
            def _():
                for kind in (SEND_P, FWD_PO, FWD_PF, FWD_PD):
                    u_copy(kind, ci).wait_recv()

                @pl.when(first)
                def _():
                    r_copy(R_OWN, ci).wait_recv()

                    @pl.when(ci + 2 < chunks)
                    def _():
                        r_copy(R_X, ci + 2).start()
                        r_copy(R_OWN, ci + 2).start()

                @pl.when(ci + 2 < chunks)
                def _():
                    u_copy(SEND_O, ci + 2).start()

            @pl.when(jnp.logical_and(kg == 1, ci + 1 < chunks))
            def _():
                @pl.when(first)
                def _():
                    r_copy(R_X, ci + 1).wait_recv()
                    r_copy(R_Y, ci + 1).start()
                    r_copy(R_PX, ci + 1).start()
                u_copy(SEND_O, ci + 1).wait_recv()
                u_copy(FWD_D, ci + 1).start()
                u_copy(FWD_PO, ci + 1).start()

                @pl.when(ci + 2 < chunks)
                def _():
                    u_copy(SEND_F, ci + 2).start()
                    u_copy(SEND_P, ci + 2).start()

            @pl.when(jnp.logical_and(kg == 2, ci + 1 < chunks))
            def _():
                u_copy(SEND_F, ci + 1).wait_recv()
                u_copy(FWD_PF, ci + 1).start()

            @pl.when(jnp.logical_and(kg == 3, ci + 1 < chunks))
            def _():
                u_copy(FWD_D, ci + 1).wait_recv()
                u_copy(FWD_PD, ci + 1).start()

                @pl.when(first)
                def _():
                    r_copy(R_Y, ci + 1).wait_recv()
                    r_copy(R_PY, ci + 1).start()

            @pl.when(jnp.logical_and(first, kg == 2))
            def _():
                r_copy(R_PX, ci).wait_recv()
                r_copy(R_PY, ci).wait_recv()

            @pl.when(jnp.logical_and(first, ci == 0))
            def _():
                for g in range(3):
                    @pl.when(kg == g + 1)
                    def _():
                        l_copy(g).wait_recv()

            r_load_wait(slot)
            last = jnp.logical_and(step == STEPS - 1, it == groups * chunks - 1)

            @pl.when(jnp.logical_not(last))
            def _():
                nit = (it + 1) % (groups * chunks)
                r_load(nit // groups, nit % groups, 1 - slot)

            left = lvm[kg].reshape(group_terms * slab, bond)
            for qp in range(phys // 2):
                o = jnp.dot(left, uvec[ci, qp], preferred_element_type=F32).astype(BF)
                xbuf[2 * qp] = o[:, :LANE]
                xbuf[2 * qp + 1] = o[:, LANE:]
            for k in range(group_terms):
                for ap in range(slab // 32):
                    r0 = k * slab + ap * 32
                    xa = xbuf[:, r0:r0 + 16, :].reshape(16 * phys, LANE)
                    xb = xbuf[:, r0 + 16:r0 + 32, :].reshape(16 * phys, LANE)
                    y = jnp.dot(kvm[kg, k], jnp.concatenate([xa, xb], axis=1), preferred_element_type=F32).astype(BF)
                    ybuf[:, ap * 32:ap * 32 + 16, k * LANE:(k + 1) * LANE] = y[:, :LANE].reshape(phys, 16, LANE)
                    ybuf[:, ap * 32 + 16:ap * 32 + 32, k * LANE:(k + 1) * LANE] = y[:, LANE:].reshape(phys, 16, LANE)
            vecs[nxt] += jnp.dot(ybuf[...].reshape(phys * slab, group_terms * LANE),
                                 rvm[slot].reshape(group_terms * LANE, bond),
                                 preferred_element_type=F32).reshape(phys, slab, bond)
            return 0
        lax.fori_loop(0, groups * chunks, iteration, 0)

        def drain(ci, _):
            for kind in range(7):
                u_copy(kind, ci).wait_send()

            @pl.when(step == 0)
            def _():
                for kind in range(5):
                    r_copy(kind, ci).wait_send()
            return 0
        lax.fori_loop(0, chunks, drain, 0)

        @pl.when(step == 0)
        def _():
            for g in range(3):
                l_copy(g).wait_send()

        def dot_q(q, acc):
            return acc + fold_tiles(vecs[nxt, q] * vecs[cur, q])
        alpha = all_mean(0, lax.fori_loop(0, phys, dot_q, jnp.zeros((8, LANE), F32)))
        beta_prev = beta_s[0:1, 0:1]

        @pl.when(step == 0)
        def _():
            def upd_q(q, _):
                vecs[nxt, q] = vecs[nxt, q] - alpha * vecs[cur, q]
                return 0
            lax.fori_loop(0, phys, upd_q, 0)

        @pl.when(step > 0)
        def _():
            def upd_q(q, _):
                vecs[nxt, q] = vecs[nxt, q] - alpha * vecs[cur, q] - beta_prev * vecs[prev, q]
                return 0
            lax.fori_loop(0, phys, upd_q, 0)

        def sq_nxt(q, acc):
            val = vecs[nxt, q]
            return acc + fold_tiles(val * val)
        beta = jnp.sqrt(all_mean(1, lax.fori_loop(0, phys, sq_nxt, jnp.zeros((8, LANE), F32))))
        beta_s[...] = jnp.broadcast_to(beta, beta_s.shape)
        ab_ref[pl.ds(step, 1), :] = jnp.broadcast_to(alpha, (1, LANE))
        ab_ref[pl.ds(8 + step, 1), :] = jnp.broadcast_to(beta, (1, LANE))
        inv = 1.0 / beta

        @pl.when(step < STEPS - 1)
        def _():
            norm_and_pack(nxt, inv, True)

        @pl.when(step == STEPS - 1)
        def _():
            norm_and_pack(nxt, inv, False)
        out_copy(nxt, step + 1).start()
        return 0
    ab_ref[...] = jnp.zeros_like(ab_ref)
    lax.fori_loop(0, STEPS, step_body, 0)
    for idx in range(STEPS - 2, STEPS + 1):
        out_copy(idx % 3, idx).wait()


def solution(mesh):
    def local_run(psi_blk, left_env, two_site, right_env):
        slab, s1, s2, bond = psi_blk.shape
        phys = s1 * s2
        terms = left_env.shape[0]
        chunks = bond // LANE
        psi = psi_blk.reshape(slab, phys, bond).transpose(1, 0, 2)
        t = lax.axis_index("terms")
        every_w = lax.all_gather(two_site, "terms", axis=0)
        xn = (1 - t // 2) * 2 + t % 2
        order = jnp.stack([t, t + 1 - 2 * (t % 2), xn, xn + 1 - 2 * (t % 2)])
        w_loc = jnp.take(every_w, order, axis=0)
        eye = jnp.eye(16, dtype=BF)
        kron = (w_loc[:, :, :, None, :, None] * eye[None, None, None, :, None, :]).reshape(4, terms, 16 * phys, 16 * phys)
        any_spec = pl.BlockSpec(memory_space=pl.ANY)
        dma = pltpu.SemaphoreType.DMA
        out, ab, _ = pl.pallas_call(
            lanczos_kernel,
            out_shape=(jax.ShapeDtypeStruct((STEPS + 1, phys, slab, bond), F32),
                       jax.ShapeDtypeStruct((16, LANE), F32),
                       jax.ShapeDtypeStruct((3, terms, bond, bond), BF)),
            in_specs=[any_spec] * 4,
            out_specs=(any_spec, pl.BlockSpec(memory_space=pltpu.VMEM), any_spec),
            scratch_shapes=[
                pltpu.VMEM((3, phys, slab, bond), F32),
                pltpu.VMEM((chunks, phys // 2, bond, 2 * LANE), BF),
                pltpu.VMEM((4, terms, slab, bond), BF),
                pltpu.VMEM((4, terms, 16 * phys, 16 * phys), BF),
                pltpu.VMEM((2, terms, LANE, bond), BF),
                pltpu.VMEM((phys, terms * slab, LANE), BF),
                pltpu.VMEM((phys, slab, terms * LANE), BF),
                pltpu.VMEM((2, 8, 8, LANE), F32),
                pltpu.VMEM((8, LANE), F32),
                dma((3,)), dma((2,)), dma((3,)),
                dma((7, chunks)), dma((7, chunks)), dma((5, chunks)), dma((5, chunks)),
                dma((3,)), dma((3,)), dma((2, 7)), dma((2, 7)),
            ],
            compiler_params=pltpu.CompilerParams(collective_id=0, has_side_effects=True, vmem_limit_bytes=60 * 2**20),
            name="lanczos",
        )(psi, left_env, kron, right_env)
        vectors = out.transpose(0, 2, 1, 3).reshape(STEPS + 1, slab, s1, s2, bond)
        return vectors, ab[:STEPS, 0], ab[8:8 + STEPS, 0]

    return jax.shard_map(local_run, mesh=mesh, in_specs=(P(("rows", "terms")), P("terms", "rows"), P("terms"), P("terms")),
                         out_specs=(P(None, ("rows", "terms")), P(), P()), check_vma=False)
```

time: 3660 us -> 1040 us (0.28)
  waiting for transfers between devices: 1330 us -> 0 us
  Pallas kernels: 0 us -> 954 us
  matrix products: 895 us -> 0 us
  local copies, waits for them, and re-layouts: 907 us -> 76.7 us
  blocking collectives: 307 us -> 10.2 us
  other arithmetic: 176 us -> 2.16 us
    pallas_call x0 -> x1, Pallas kernels: none -> 954 us  [local_run(): pl.pallas_call(lanczos_kernel, out_shape=(jax.ShapeDtypeStruct((STEPS + 1...]
    dot_general x18 -> x0, matrix products: 895 us -> none  [the longest x6 339 us: matvec(): left_out = jnp.dot(left_flat, flat_vec, preferred_element_type=jnp.float32)]
    reduce_scatter x6 -> x0, waiting for transfers between devices: 768 us -> none  [matvec(): lax.psum_scatter(part_sum, 'terms', scatter_dimension=0, tiled=True)]
    all_gather x6 -> x0, waiting for transfers between devices: 564 us -> none  [matvec(): lax.all_gather(cur_blk.astype(jnp.bfloat16), all_axes, axis=0, tiled=True)]
    convert_element_type x6 -> x0, local copies, waits for them, and re-layouts: 394 us -> none  [matvec(): left_out.astype(jnp.bfloat16)]
    psum x13 -> x0, blocking collectives: 307 us -> none  [inner_mean(): return lax.psum(jnp.sum(x_vec * y_vec), all_axes) / elem_count]
    unnamed x19 -> x4, local copies, waits for them, and re-layouts: 232 us -> 37.1 us
    reshape x6 -> x0, local copies, waits for them, and re-layouts: 175 us -> none  [matvec(): flat_vec = whole_vec.reshape(bond_dim, phys_pair * bond_dim)]
  transfers between devices with their start and end apart: 12 -> 0, of which waited for: 12 -> 0; matrix products, arithmetic and copies ran while one was open for 1% -> 0% of each run, Pallas kernels for 0% -> 0%
where the time goes in v1:
time: 1040 us
  Pallas kernels  954 us (92%)
  local copies, waits for them, and re-layouts  76.7 us (7%)
    pallas_call x1, Pallas kernels, local_run(): pl.pallas_call(lanczos_kernel, out_shape=(jax.ShapeDtypeStruct((STEPS + 1...  954 us
    mul x4, local copies, waits for them, and re-layouts, local_run(): w_loc[:, :, :, None, :, None] * eye[None, None, None, :, None, :]  38.4 us
    unnamed x4, local copies, waits for them, and re-layouts  37.1 us

profile of v1, /device:TPU:0, one launch (start us, length us, event | category | flops | bytes accessed | tf_op | source)
XLA Modules:
  0.0 1043.5 jit_solution(17309769463731369054)
XLA Ops:
  0.7 0.1 compare_and_fusion
  0.7 0.1 fusion.1
  0.8 10.2 all-gather
  11.0 0.6 gather_fusion
  11.6 0.1 broadcast_select_fusion
  11.6 0.2 mul.31
  11.9 1.0 mul.32
  12.8 7.2 copy.11
  20.0 8.7 mul.29
  28.8 28.5 %mul.30 = bf16[4,6,256,256]{3,2,1,0:T(8,128)(2,1)S(1)} reshape(bf16[4,6,16,16,16,16]{5,4,3,2,1,0:T(8,128)(2,1)} %mul.29) | data formatting | bytes 6291456 | tf_op jit(solution)/shard_map/mul | solution.py:377
  57.3 1.9 broadcast_multiply_fusion.kron_ref
  59.2 953.8 %lanczos.1 = (f32[7,16,96,768]{3,2,1,0:T(8,128)}, f32[16,128]{1,0:T(8,128)}, bf16[3,6,768,768]{3,2,1,0:T(8,128)(2,1)}) custom-call(f32[16,96,768]{2,1,0:T(8,128)} %bitcast.22, bf16[6,384,768]{2,1,0:T(8,128)(2,1)} %left_ref.1, bf16[4,6,256,256]{3,2,1,0:T(8,128)(2,1)} %broadcast_multiply_fusion.kron_ref, bf16[6,768,768]{2,1,0:T(8,128)(2,1)} %right_ref.1), custom_call_target="tpu_custom_call" | custom-call | tf_op jit(solution)/shard_map/lanczos/pallas_call | solution.py:380
  1013.0 0.0 copy-start
  1013.0 29.9 %copy.12 = f32[7,96,4,4,768]{4,3,2,1,0:T(4,128)} copy(f32[7,96,4,4,768]{4,1,3,2,0:T(8,128)} %bitcast.21) | data formatting | bytes 66060288
  1042.9 0.0 copy-done
  1042.9 0.7 slice_reduce_fusion
  (2 shorter events, 0.0 us)
Async XLA Ops:
  1013.0 29.9 %copy-start = (f32[16,128]{1,0:T(8,128)S(1)}, f32[16,128]{1,0:T(8,128)}, u32[]{:S(2)}) copy-start(f32[16,128]{1,0:T(8,128)} %get-tuple-element.6) | copy-start | bytes 24580
